TPU v7x, 32 devices: a whole 2x2x4 slice. The times are simulated.
32 devices in a mesh: section: 4 (over z), batch: 2 (over x), tile: 4 (over y, core).
Axes of the slice: x: 2, y: 2, z: 4, core: 2. Of those that a mesh axis runs over, the one named last changes fastest.
Arguments:
- latents: bfloat16 [8, 4, 32, 1280], P('batch', 'tile'), parts along dimension 0, may hold values from -6 to 6
- prompt_tokens: bfloat16 [8, 77, 2048], P('batch'), parts along dimension 0, may hold values from -6 to 6
- fresh_noise: bfloat16 [1, 8, 4, 32, 1280], P(None, 'batch', 'tile'), parts along dimension 1, may hold values from -6 to 6
- timesteps: int32 [2], replicated, may hold values from 600 to 999
- entry_order: int32 [8], P('batch'), parts along dimension 0, may hold values from 0 to 3, each once
- timestep_weight: bfloat16 [4, 320, 1280], P('section'), may hold values from -0.3125 to 0.3125
- conv_kernel: float32 [4, 9, 1280], P('section'), may hold values from -1 to 1
- norm_gain: float32 [4, 1280], P('section'), may hold values from 0.25 to 1.75
- layer_norm_bias: float32 [4, 1280], P('section'), may hold values from -1.5 to 1.5
- qkv_weight: bfloat16 [4, 1280, 3, 1280], P('section', None, None, 'tile'), may hold values from -0.15625 to 0.15625
- prompt_weight: bfloat16 [4, 2048, 2, 1280], P('section', None, None, 'tile'), may hold values from -0.125 to 0.125
- out_weight: bfloat16 [4, 1280, 1280], P('section', 'tile'), may hold values from -0.15625 to 0.15625
Outputs:
- samples: bfloat16 [8, 4, 32, 1280], P('batch', 'tile', None, 'section'), parts along dimension 0
There are 2 independent parts, one for each index of `batch`. A program takes and returns all parts, laid end to end along the dimension named above; an argument that names none is the same for every part. Nothing has to cross between parts.
All inputs are finite; a program needn't handle non-finite values.
Results may differ from a plain program's by a relative error of at most 0.019.
Values may be sent and summed in bfloat16 or wider, within the bound.
A program may use at most 64 MiB of HBM per device.

v0:
```python
import math
import jax
import jax.numpy as jnp
from jax import lax
from jax.sharding import PartitionSpec as P

HEADS = 20


def extended(cells, sides, width):
    for axis, dim in sides:
        count = lax.axis_size(axis)
        ends = count - 1
        head = lax.slice_in_dim(cells, 0, width, axis=dim)
        tail = lax.slice_in_dim(cells, cells.shape[dim] - width, cells.shape[dim], axis=dim)
        cells = jnp.concatenate(
            [
                lax.ppermute(tail, axis, [(i, (i + 1) % count) for i in range(ends)]),
                cells,
                lax.ppermute(head, axis, [((i + 1) % count, i) for i in range(ends)]),
            ],
            axis=dim,
        )
    return cells


def from_behind(shard, axis, by):
    count = lax.axis_size(axis)
    return lax.ppermute(shard, axis, [(i, (i + by) % count) for i in range(count)])


def spread_2(shard, axis, root):
    mine = lax.axis_index(axis) == root
    return lax.psum(jnp.where(mine, shard, jnp.zeros_like(shard)), axis)


def noise_plan():
    positions = jnp.arange(1000, dtype=jnp.float32)
    low_root = math.sqrt(0.00085)
    high_root = math.sqrt(0.012)
    roots = low_root + (high_root - low_root) * positions / 999.0
    return jnp.exp(jnp.cumsum(jnp.log(1.0 - roots * roots)))


def time_features(timesteps, half_count):
    exponents = jnp.arange(half_count, dtype=jnp.float32) / half_count
    freq_row = jnp.exp(-math.log(10000.0) * exponents)
    angles = timesteps.astype(jnp.float32)[:, None] * freq_row[None, :]
    return jnp.concatenate([jnp.cos(angles), jnp.sin(angles)], axis=1).astype(jnp.bfloat16)


def pick_scalar(alpha_table, position):
    hits = jnp.arange(alpha_table.shape[0], dtype=jnp.int32) == position
    return jnp.sum(jnp.where(hits, alpha_table, jnp.zeros_like(alpha_table)))


def pick_integer(int_table, position):
    hits = jnp.arange(int_table.shape[0], dtype=jnp.int32) == position
    return jnp.sum(jnp.where(hits, int_table, jnp.zeros_like(int_table)))


def mix_positions(rimmed, kernel_body):
    row_total = rimmed.shape[0] - 2
    col_total = rimmed.shape[1]
    framed = jnp.pad(rimmed.astype(jnp.float32), ((0, 0), (1, 1), (0, 0)))
    mixed = rimmed[1:-1].astype(jnp.float32)
    for offset_row in range(3):
        for offset_col in range(3):
            mixed = (
                mixed
                + kernel_body[3 * offset_row + offset_col]
                * framed[offset_row : offset_row + row_total, offset_col : offset_col + col_total]
            )
    return mixed


def layer_norm(values_in, scale_row, shift_row):
    centre = jnp.mean(values_in, axis=-1, keepdims=True)
    spread = jnp.mean(jnp.square(values_in - centre), axis=-1, keepdims=True)
    return (values_in - centre) * lax.rsqrt(spread + 1e-05) * scale_row + shift_row


def attend(queries, keys_all, values_all, head_count):
    query_count = queries.shape[0]
    key_count = keys_all.shape[0]
    head_width = queries.shape[1] // head_count
    query_heads = queries.reshape(query_count, head_count, head_width)
    key_heads = keys_all.reshape(key_count, head_count, head_width)
    value_heads = values_all.reshape(key_count, head_count, head_width)
    scores = jnp.einsum(
        "qhd,khd->hqk", query_heads, key_heads, preferred_element_type=jnp.float32
    ) / math.sqrt(head_width)
    powers = jnp.exp(scores)
    soft_weights = (powers / jnp.sum(powers, axis=-1, keepdims=True)).astype(jnp.bfloat16)
    attended = jnp.einsum(
        "hqk,khd->qhd", soft_weights, value_heads, preferred_element_type=jnp.float32
    )
    return attended.reshape(query_count, head_count * head_width).astype(jnp.bfloat16)


def per_device(
    latents,
    prompt_tokens,
    fresh_noise,
    timesteps,
    entry_order,
    timestep_weight,
    conv_kernel,
    norm_gain,
    layer_norm_bias,
    qkv_weight,
    prompt_weight,
    out_weight,
):
    section_count = lax.axis_size("section")
    tile_count = lax.axis_size("tile")
    section_index = lax.axis_index("section")
    micro_count, rows_here, cols_here, width_all = latents.shape
    token_here = rows_here * cols_here
    chain_total = timesteps.shape[0]
    alpha_table = noise_plan()
    feature_rows = time_features(timesteps, timestep_weight.shape[1] // 2)
    timestep_embedding_all = jnp.dot(
        feature_rows, timestep_weight[0], preferred_element_type=jnp.float32
    )
    kernel_body = conv_kernel[0]
    scale_row = norm_gain[0]
    shift_row = layer_norm_bias[0]
    qkv_local = qkv_weight[0]
    prompt_local = prompt_weight[0]
    out_local = out_weight[0]
    local_heads = HEADS // tile_count
    micro_ids = jnp.arange(micro_count, dtype=jnp.int32)

    def prompt_for(latent_id):
        prompt_row = lax.dynamic_index_in_dim(prompt_tokens, latent_id, 0, False)
        local_pair = jnp.einsum(
            "tc,cjd->tjd", prompt_row, prompt_local, preferred_element_type=jnp.float32
        ).astype(jnp.bfloat16)
        return local_pair

    def lift_and_mix(current, temb_row):
        lifted = (current.astype(jnp.float32) + temb_row).astype(jnp.bfloat16)
        rimmed = extended(lifted, (("tile", 0),), 1)
        mixed = mix_positions(rimmed, kernel_body).reshape(token_here, width_all)
        normed = layer_norm(mixed, scale_row, shift_row).astype(jnp.bfloat16)
        return (mixed, normed)

    def section_heads(current, temb_row, prompt_pair):
        mixed, normed = lift_and_mix(current, temb_row)
        normed_all = lax.all_gather(normed, "tile", axis=0, tiled=True)
        projected = jnp.einsum(
            "tc,cjd->tjd", normed_all, qkv_local, preferred_element_type=jnp.float32
        ).astype(jnp.bfloat16)
        keys_all = jnp.concatenate([projected[:, 1], prompt_pair[:, 0]], axis=0)
        values_all = jnp.concatenate([projected[:, 2], prompt_pair[:, 1]], axis=0)
        attended = attend(projected[:, 0], keys_all, values_all, local_heads)
        update = lax.psum_scatter(
            jnp.dot(attended, out_local, preferred_element_type=jnp.float32).astype(jnp.bfloat16),
            "tile",
            scatter_dimension=0,
            tiled=True,
        ).astype(jnp.float32)
        return (mixed + update).astype(jnp.bfloat16).reshape(rows_here, cols_here, width_all)

    def advance(tick_counter, state_pair):
        carried_state, results = state_pair
        incoming = from_behind(carried_state, "section", 1)
        offset = tick_counter - section_index
        chain_level = jnp.floor_divide(offset, section_count)
        slot_index = offset - chain_level * section_count
        active = (offset >= 0) & (chain_level < chain_total) & (slot_index < micro_count)
        level_clip = jnp.clip(chain_level, 0, chain_total - 1)
        slot_clip = jnp.clip(slot_index, 0, micro_count - 1)
        noise_clip = jnp.clip(chain_level - 1, 0, chain_total - 2)
        latent_id = pick_integer(entry_order, slot_clip)
        starting = lax.dynamic_index_in_dim(latents, latent_id, 0, False)
        noise_slab = lax.dynamic_index_in_dim(
            lax.dynamic_index_in_dim(fresh_noise, noise_clip, 0, False), slot_clip, 0, False
        )
        alpha_bar = pick_scalar(alpha_table, pick_integer(timesteps, level_clip))
        renoised = (
            jnp.sqrt(alpha_bar) * incoming.astype(jnp.float32)
            + jnp.sqrt(1.0 - alpha_bar) * noise_slab.astype(jnp.float32)
        ).astype(jnp.bfloat16)
        first_section = section_index == 0
        current = jnp.where(
            first_section & (chain_level == 0),
            starting,
            jnp.where(first_section, renoised, incoming),
        )
        temb_row = lax.dynamic_index_in_dim(timestep_embedding_all, level_clip, 0, False)
        prompt_pair = prompt_for(latent_id)
        computed = section_heads(current, temb_row, prompt_pair)
        produced = jnp.where(active, computed, jnp.zeros_like(computed))
        finishing = active & (section_index == section_count - 1) & (chain_level == chain_total - 1)
        placing = finishing & (micro_ids == latent_id)
        results = jnp.where(placing[:, None, None, None], produced[None], results)
        return (produced, results)

    tick_total = chain_total * section_count + micro_count - 1
    initial_latent = (
        jnp.zeros((rows_here, cols_here, width_all), jnp.bfloat16),
        jnp.zeros_like(latents),
    )
    final_state = lax.fori_loop(0, tick_total, advance, initial_latent)
    gathered = spread_2(final_state[1], "section", section_count - 1)
    share_width = width_all // section_count
    return lax.dynamic_slice_in_dim(gathered, section_index * share_width, share_width, 3)


def solution(mesh):
    placed = (
        P("batch", "tile", None, None),
        P("batch", None, None),
        P(None, "batch", "tile", None, None),
        P(),
        P("batch"),
        P("section", None, None),
        P("section", None, None),
        P("section", None),
        P("section", None),
        P("section", None, None, "tile"),
        P("section", None, None, "tile"),
        P("section", "tile", None),
    )
    return jax.shard_map(
        per_device,
        mesh=mesh,
        in_specs=placed,
        out_specs=P("batch", "tile", None, "section"),
        check_vma=False,
    )
```

profile of v0, /device:TPU:0, one launch (start us, length us, event | category | flops | bytes accessed | tf_op | source)
XLA Modules:
  0.0 719.2 jit_solution(13876428785944258102)
XLA Ops:
  9.0 3.1 copy.18
  14.4 656.9 %while.18 = (s32[]{:T(128)}, bf16[1,32,1280]{2,1,0:T(8,128)(2,1)}, bf16[4,1,32,1280]{3,2,1,0:T(8,128)(2,1)}, s32[]{:T(128)}, pred[]{:T(512)}, /*index=5*/s32[4]{...) while((s32[]{:T(128)}, bf16[1,32,1280]{2,1,0:T(8,128)(2,1)}, ...), condition=%wide.region_10.11_spmd.clone, body=%wide.region_2.10_spmd.clone.sunk | while | flops 658625344 | bytes 26783188 | solution.py:206
  14.5 3.1 collective-permute-start
  32.6 3.0 collective-permute-start.2
  37.7 8.1 %all_gather.12 = bf16[128,1280]{1,0:T(8,128)(2,1)S(1)} all-gather(bf16[32,1280]{1,0:T(8,128)(2,1)S(1)} %add_convert_fusion.5), channel_id=1, replica_groups=mesh['section'=4,'batch'=2,'tile'=4] {'tile'}, dimensions={0}, use_global_device_ids=true | all-gather | bytes 409600 | tf_op jit(solution)/shard_map/while/body/eval_jaxpr/all_gather | solution.py:151
  50.0 2.3 convolution_convert_fusion.11
  52.9 19.9 %reduce-scatter.2.cloned.1.call-done = bf16[32,1280]{1,0:T(8,128)(2,1)} async-done(((bf16[128,1280]{1,0:T(8,128)(2,1)}), bf16[32,1280]{1,0:T(8,128)(2,1)}) %reduce-scatter.2.cloned.1.call-update) | async-done | bytes 81936 | tf_op jit(solution)/shard_map/while/body/eval_jaxpr/reduce_scatter | solution.py:158
  92.7 3.0 collective-permute-start.2
  97.8 7.5 %all_gather.12 = bf16[128,1280]{1,0:T(8,128)(2,1)S(1)} all-gather(bf16[32,1280]{1,0:T(8,128)(2,1)S(1)} %add_convert_fusion.5), channel_id=1, replica_groups=mesh['section'=4,'batch'=2,'tile'=4] {'tile'}, dimensions={0}, use_global_device_ids=true | all-gather | bytes 409600 | tf_op jit(solution)/shard_map/while/body/eval_jaxpr/all_gather | solution.py:151
  109.5 2.3 convolution_convert_fusion.11
  112.5 19.8 %reduce-scatter.2.cloned.1.call-done = bf16[32,1280]{1,0:T(8,128)(2,1)} async-done(((bf16[128,1280]{1,0:T(8,128)(2,1)}), bf16[32,1280]{1,0:T(8,128)(2,1)}) %reduce-scatter.2.cloned.1.call-update) | async-done | bytes 81936 | tf_op jit(solution)/shard_map/while/body/eval_jaxpr/reduce_scatter | solution.py:158
  152.3 3.0 collective-permute-start.2
  157.4 7.6 %all_gather.12 = bf16[128,1280]{1,0:T(8,128)(2,1)S(1)} all-gather(bf16[32,1280]{1,0:T(8,128)(2,1)S(1)} %add_convert_fusion.5), channel_id=1, replica_groups=mesh['section'=4,'batch'=2,'tile'=4] {'tile'}, dimensions={0}, use_global_device_ids=true | all-gather | bytes 409600 | tf_op jit(solution)/shard_map/while/body/eval_jaxpr/all_gather | solution.py:151
  169.1 2.3 convolution_convert_fusion.11
  172.1 19.8 %reduce-scatter.2.cloned.1.call-done = bf16[32,1280]{1,0:T(8,128)(2,1)} async-done(((bf16[128,1280]{1,0:T(8,128)(2,1)}), bf16[32,1280]{1,0:T(8,128)(2,1)}) %reduce-scatter.2.cloned.1.call-update) | async-done | bytes 81936 | tf_op jit(solution)/shard_map/while/body/eval_jaxpr/reduce_scatter | solution.py:158
  211.8 3.0 collective-permute-start.2
  216.9 7.6 %all_gather.12 = bf16[128,1280]{1,0:T(8,128)(2,1)S(1)} all-gather(bf16[32,1280]{1,0:T(8,128)(2,1)S(1)} %add_convert_fusion.5), channel_id=1, replica_groups=mesh['section'=4,'batch'=2,'tile'=4] {'tile'}, dimensions={0}, use_global_device_ids=true | all-gather | bytes 409600 | tf_op jit(solution)/shard_map/while/body/eval_jaxpr/all_gather | solution.py:151
  228.6 2.3 convolution_convert_fusion.11
  231.6 19.8 %reduce-scatter.2.cloned.1.call-done = bf16[32,1280]{1,0:T(8,128)(2,1)} async-done(((bf16[128,1280]{1,0:T(8,128)(2,1)}), bf16[32,1280]{1,0:T(8,128)(2,1)}) %reduce-scatter.2.cloned.1.call-update) | async-done | bytes 81936 | tf_op jit(solution)/shard_map/while/body/eval_jaxpr/reduce_scatter | solution.py:158
  271.3 3.0 collective-permute-start.2
  276.4 7.6 %all_gather.12 = bf16[128,1280]{1,0:T(8,128)(2,1)S(1)} all-gather(bf16[32,1280]{1,0:T(8,128)(2,1)S(1)} %add_convert_fusion.5), channel_id=1, replica_groups=mesh['section'=4,'batch'=2,'tile'=4] {'tile'}, dimensions={0}, use_global_device_ids=true | all-gather | bytes 409600 | tf_op jit(solution)/shard_map/while/body/eval_jaxpr/all_gather | solution.py:151
  288.1 2.3 convolution_convert_fusion.11
  291.1 19.8 %reduce-scatter.2.cloned.1.call-done = bf16[32,1280]{1,0:T(8,128)(2,1)} async-done(((bf16[128,1280]{1,0:T(8,128)(2,1)}), bf16[32,1280]{1,0:T(8,128)(2,1)}) %reduce-scatter.2.cloned.1.call-update) | async-done | bytes 81936 | tf_op jit(solution)/shard_map/while/body/eval_jaxpr/reduce_scatter | solution.py:158
  330.8 3.0 collective-permute-start.2
  335.9 7.5 %all_gather.12 = bf16[128,1280]{1,0:T(8,128)(2,1)S(1)} all-gather(bf16[32,1280]{1,0:T(8,128)(2,1)S(1)} %add_convert_fusion.5), channel_id=1, replica_groups=mesh['section'=4,'batch'=2,'tile'=4] {'tile'}, dimensions={0}, use_global_device_ids=true | all-gather | bytes 409600 | tf_op jit(solution)/shard_map/while/body/eval_jaxpr/all_gather | solution.py:151
  347.6 2.3 convolution_convert_fusion.11
  350.6 19.8 %reduce-scatter.2.cloned.1.call-done = bf16[32,1280]{1,0:T(8,128)(2,1)} async-done(((bf16[128,1280]{1,0:T(8,128)(2,1)}), bf16[32,1280]{1,0:T(8,128)(2,1)}) %reduce-scatter.2.cloned.1.call-update) | async-done | bytes 81936 | tf_op jit(solution)/shard_map/while/body/eval_jaxpr/reduce_scatter | solution.py:158
  390.3 3.0 collective-permute-start.2
  395.4 7.6 %all_gather.12 = bf16[128,1280]{1,0:T(8,128)(2,1)S(1)} all-gather(bf16[32,1280]{1,0:T(8,128)(2,1)S(1)} %add_convert_fusion.5), channel_id=1, replica_groups=mesh['section'=4,'batch'=2,'tile'=4] {'tile'}, dimensions={0}, use_global_device_ids=true | all-gather | bytes 409600 | tf_op jit(solution)/shard_map/while/body/eval_jaxpr/all_gather | solution.py:151
  407.1 2.3 convolution_convert_fusion.11
  410.1 19.8 %reduce-scatter.2.cloned.1.call-done = bf16[32,1280]{1,0:T(8,128)(2,1)} async-done(((bf16[128,1280]{1,0:T(8,128)(2,1)}), bf16[32,1280]{1,0:T(8,128)(2,1)}) %reduce-scatter.2.cloned.1.call-update) | async-done | bytes 81936 | tf_op jit(solution)/shard_map/while/body/eval_jaxpr/reduce_scatter | solution.py:158
  449.8 3.0 collective-permute-start.2
  455.0 7.5 %all_gather.12 = bf16[128,1280]{1,0:T(8,128)(2,1)S(1)} all-gather(bf16[32,1280]{1,0:T(8,128)(2,1)S(1)} %add_convert_fusion.5), channel_id=1, replica_groups=mesh['section'=4,'batch'=2,'tile'=4] {'tile'}, dimensions={0}, use_global_device_ids=true | all-gather | bytes 409600 | tf_op jit(solution)/shard_map/while/body/eval_jaxpr/all_gather | solution.py:151
  466.6 2.3 convolution_convert_fusion.11
  469.6 19.8 %reduce-scatter.2.cloned.1.call-done = bf16[32,1280]{1,0:T(8,128)(2,1)} async-done(((bf16[128,1280]{1,0:T(8,128)(2,1)}), bf16[32,1280]{1,0:T(8,128)(2,1)}) %reduce-scatter.2.cloned.1.call-update) | async-done | bytes 81936 | tf_op jit(solution)/shard_map/while/body/eval_jaxpr/reduce_scatter | solution.py:158
  509.3 3.0 collective-permute-start.2
  514.5 7.5 %all_gather.12 = bf16[128,1280]{1,0:T(8,128)(2,1)S(1)} all-gather(bf16[32,1280]{1,0:T(8,128)(2,1)S(1)} %add_convert_fusion.5), channel_id=1, replica_groups=mesh['section'=4,'batch'=2,'tile'=4] {'tile'}, dimensions={0}, use_global_device_ids=true | all-gather | bytes 409600 | tf_op jit(solution)/shard_map/while/body/eval_jaxpr/all_gather | solution.py:151
  526.2 2.3 convolution_convert_fusion.11
  529.1 19.8 %reduce-scatter.2.cloned.1.call-done = bf16[32,1280]{1,0:T(8,128)(2,1)} async-done(((bf16[128,1280]{1,0:T(8,128)(2,1)}), bf16[32,1280]{1,0:T(8,128)(2,1)}) %reduce-scatter.2.cloned.1.call-update) | async-done | bytes 81936 | tf_op jit(solution)/shard_map/while/body/eval_jaxpr/reduce_scatter | solution.py:158
  568.9 3.0 collective-permute-start.2
  574.0 7.5 %all_gather.12 = bf16[128,1280]{1,0:T(8,128)(2,1)S(1)} all-gather(bf16[32,1280]{1,0:T(8,128)(2,1)S(1)} %add_convert_fusion.5), channel_id=1, replica_groups=mesh['section'=4,'batch'=2,'tile'=4] {'tile'}, dimensions={0}, use_global_device_ids=true | all-gather | bytes 409600 | tf_op jit(solution)/shard_map/while/body/eval_jaxpr/all_gather | solution.py:151
  585.7 2.3 convolution_convert_fusion.11
  588.6 19.8 %reduce-scatter.2.cloned.1.call-done = bf16[32,1280]{1,0:T(8,128)(2,1)} async-done(((bf16[128,1280]{1,0:T(8,128)(2,1)}), bf16[32,1280]{1,0:T(8,128)(2,1)}) %reduce-scatter.2.cloned.1.call-update) | async-done | bytes 81936 | tf_op jit(solution)/shard_map/while/body/eval_jaxpr/reduce_scatter | solution.py:158
  628.4 3.0 collective-permute-start.2
  633.5 7.5 %all_gather.12 = bf16[128,1280]{1,0:T(8,128)(2,1)S(1)} all-gather(bf16[32,1280]{1,0:T(8,128)(2,1)S(1)} %add_convert_fusion.5), channel_id=1, replica_groups=mesh['section'=4,'batch'=2,'tile'=4] {'tile'}, dimensions={0}, use_global_device_ids=true | all-gather | bytes 409600 | tf_op jit(solution)/shard_map/while/body/eval_jaxpr/all_gather | solution.py:151
  645.2 2.3 convolution_convert_fusion.11
  648.1 19.8 %reduce-scatter.2.cloned.1.call-done = bf16[32,1280]{1,0:T(8,128)(2,1)} async-done(((bf16[128,1280]{1,0:T(8,128)(2,1)}), bf16[32,1280]{1,0:T(8,128)(2,1)}) %reduce-scatter.2.cloned.1.call-update) | async-done | bytes 81936 | tf_op jit(solution)/shard_map/while/body/eval_jaxpr/reduce_scatter | solution.py:158
  672.1 38.3 %all-reduce.4.cloned.1.call-done = bf16[4,1,32,1280]{3,2,1,0:T(8,128)(2,1)} async-done(((bf16[4,1,32,1280]{3,2,1,0:T(8,128)(2,1)}), bf16[4,1,32,1280]{3,2,1,0:T(8,128)(2,1)}) %all-reduce.4.cloned.1.call-update) | async-done | bytes 327696 | tf_op jit(solution)/shard_map/psum | solution.py:34
  (448 shorter events, 262.5 us)
Async XLA Ops:
  14.4 58.4 %reduce-scatter.2.cloned.1.call-start = ((), (), s32[]{:S(2)}) async-start(), calls=%async_computation.2 | async-start | bytes 409600 | tf_op jit(solution)/shard_map/while/body/eval_jaxpr/reduce_scatter | solution.py:158
  14.5 15.8 %collective-permute-start = (bf16[1,32,1280]{2,1,0:T(8,128)(2,1)}, bf16[1,32,1280]{2,1,0:T(8,128)(2,1)}, u32[]{:S(2)}, u32[]{:S(2)}) collective-permute-start(bf16[1,32,1280]{2,1,0:T(8,128)(2,1)} %get-tuple-element.768), channel_id=1, source_target_pairs={{0,8},{8,16},{16,24},{24,0},{1,9},{9,17},{17,25},{25,1},{2,10},{10... | collective-permute-start | bytes 245768 | tf_op jit(solution)/shard_map/while/body/eval_jaxpr/ppermute | solution.py:29
  31.3 5.7 collective-permute-start.1
  32.6 4.5 collective-permute-start.2
  48.4 27.8 %copy-start.6 = (f32[1,1280]{1,0:T(1,128)S(1)}, f32[1,1280]{1,0:T(1,128)}, u32[]{:S(2)}) copy-start(f32[1,1280]{1,0:T(1,128)} %get-tuple-element.859) | copy-start | bytes 15364 | tf_op jit(solution)/shard_map/while
  76.2 56.1 %reduce-scatter.2.cloned.1.call-start = ((), (), s32[]{:S(2)}) async-start(), calls=%async_computation.2 | async-start | bytes 409600 | tf_op jit(solution)/shard_map/while/body/eval_jaxpr/reduce_scatter | solution.py:158
  76.2 14.2 %collective-permute-start = (bf16[1,32,1280]{2,1,0:T(8,128)(2,1)}, bf16[1,32,1280]{2,1,0:T(8,128)(2,1)}, u32[]{:S(2)}, u32[]{:S(2)}) collective-permute-start(bf16[1,32,1280]{2,1,0:T(8,128)(2,1)} %get-tuple-element.768), channel_id=1, source_target_pairs={{0,8},{8,16},{16,24},{24,0},{1,9},{9,17},{17,25},{25,1},{2,10},{10... | collective-permute-start | bytes 245768 | tf_op jit(solution)/shard_map/while/body/eval_jaxpr/ppermute | solution.py:29
  91.4 5.7 collective-permute-start.1
  92.7 4.5 collective-permute-start.2
  108.0 27.7 %copy-start.6 = (f32[1,1280]{1,0:T(1,128)S(1)}, f32[1,1280]{1,0:T(1,128)}, u32[]{:S(2)}) copy-start(f32[1,1280]{1,0:T(1,128)} %get-tuple-element.859) | copy-start | bytes 15364 | tf_op jit(solution)/shard_map/while
  135.7 56.1 %reduce-scatter.2.cloned.1.call-start = ((), (), s32[]{:S(2)}) async-start(), calls=%async_computation.2 | async-start | bytes 409600 | tf_op jit(solution)/shard_map/while/body/eval_jaxpr/reduce_scatter | solution.py:158
  135.7 14.2 %collective-permute-start = (bf16[1,32,1280]{2,1,0:T(8,128)(2,1)}, bf16[1,32,1280]{2,1,0:T(8,128)(2,1)}, u32[]{:S(2)}, u32[]{:S(2)}) collective-permute-start(bf16[1,32,1280]{2,1,0:T(8,128)(2,1)} %get-tuple-element.768), channel_id=1, source_target_pairs={{0,8},{8,16},{16,24},{24,0},{1,9},{9,17},{17,25},{25,1},{2,10},{10... | collective-permute-start | bytes 245768 | tf_op jit(solution)/shard_map/while/body/eval_jaxpr/ppermute | solution.py:29
  151.0 5.7 collective-permute-start.1
  152.3 4.5 collective-permute-start.2
  195.3 56.1 %reduce-scatter.2.cloned.1.call-start = ((), (), s32[]{:S(2)}) async-start(), calls=%async_computation.2 | async-start | bytes 409600 | tf_op jit(solution)/shard_map/while/body/eval_jaxpr/reduce_scatter | solution.py:158
  195.3 14.1 %collective-permute-start = (bf16[1,32,1280]{2,1,0:T(8,128)(2,1)}, bf16[1,32,1280]{2,1,0:T(8,128)(2,1)}, u32[]{:S(2)}, u32[]{:S(2)}) collective-permute-start(bf16[1,32,1280]{2,1,0:T(8,128)(2,1)} %get-tuple-element.768), channel_id=1, source_target_pairs={{0,8},{8,16},{16,24},{24,0},{1,9},{9,17},{17,25},{25,1},{2,10},{10... | collective-permute-start | bytes 245768 | tf_op jit(solution)/shard_map/while/body/eval_jaxpr/ppermute | solution.py:29
  210.5 5.7 collective-permute-start.1
  211.8 4.5 collective-permute-start.2
  254.8 56.1 %reduce-scatter.2.cloned.1.call-start = ((), (), s32[]{:S(2)}) async-start(), calls=%async_computation.2 | async-start | bytes 409600 | tf_op jit(solution)/shard_map/while/body/eval_jaxpr/reduce_scatter | solution.py:158
  254.8 14.1 %collective-permute-start = (bf16[1,32,1280]{2,1,0:T(8,128)(2,1)}, bf16[1,32,1280]{2,1,0:T(8,128)(2,1)}, u32[]{:S(2)}, u32[]{:S(2)}) collective-permute-start(bf16[1,32,1280]{2,1,0:T(8,128)(2,1)} %get-tuple-element.768), channel_id=1, source_target_pairs={{0,8},{8,16},{16,24},{24,0},{1,9},{9,17},{17,25},{25,1},{2,10},{10... | collective-permute-start | bytes 245768 | tf_op jit(solution)/shard_map/while/body/eval_jaxpr/ppermute | solution.py:29
  270.0 5.7 collective-permute-start.1
  271.3 4.5 collective-permute-start.2
  314.3 56.1 %reduce-scatter.2.cloned.1.call-start = ((), (), s32[]{:S(2)}) async-start(), calls=%async_computation.2 | async-start | bytes 409600 | tf_op jit(solution)/shard_map/while/body/eval_jaxpr/reduce_scatter | solution.py:158
  314.3 14.2 %collective-permute-start = (bf16[1,32,1280]{2,1,0:T(8,128)(2,1)}, bf16[1,32,1280]{2,1,0:T(8,128)(2,1)}, u32[]{:S(2)}, u32[]{:S(2)}) collective-permute-start(bf16[1,32,1280]{2,1,0:T(8,128)(2,1)} %get-tuple-element.768), channel_id=1, source_target_pairs={{0,8},{8,16},{16,24},{24,0},{1,9},{9,17},{17,25},{25,1},{2,10},{10... | collective-permute-start | bytes 245768 | tf_op jit(solution)/shard_map/while/body/eval_jaxpr/ppermute | solution.py:29
  329.5 5.7 collective-permute-start.1
  330.8 4.5 collective-permute-start.2
  373.8 56.1 %reduce-scatter.2.cloned.1.call-start = ((), (), s32[]{:S(2)}) async-start(), calls=%async_computation.2 | async-start | bytes 409600 | tf_op jit(solution)/shard_map/while/body/eval_jaxpr/reduce_scatter | solution.py:158
  373.8 14.1 %collective-permute-start = (bf16[1,32,1280]{2,1,0:T(8,128)(2,1)}, bf16[1,32,1280]{2,1,0:T(8,128)(2,1)}, u32[]{:S(2)}, u32[]{:S(2)}) collective-permute-start(bf16[1,32,1280]{2,1,0:T(8,128)(2,1)} %get-tuple-element.768), channel_id=1, source_target_pairs={{0,8},{8,16},{16,24},{24,0},{1,9},{9,17},{17,25},{25,1},{2,10},{10... | collective-permute-start | bytes 245768 | tf_op jit(solution)/shard_map/while/body/eval_jaxpr/ppermute | solution.py:29
  389.0 5.7 collective-permute-start.1
  390.3 4.5 collective-permute-start.2
  433.3 56.1 %reduce-scatter.2.cloned.1.call-start = ((), (), s32[]{:S(2)}) async-start(), calls=%async_computation.2 | async-start | bytes 409600 | tf_op jit(solution)/shard_map/while/body/eval_jaxpr/reduce_scatter | solution.py:158
  433.3 14.2 %collective-permute-start = (bf16[1,32,1280]{2,1,0:T(8,128)(2,1)}, bf16[1,32,1280]{2,1,0:T(8,128)(2,1)}, u32[]{:S(2)}, u32[]{:S(2)}) collective-permute-start(bf16[1,32,1280]{2,1,0:T(8,128)(2,1)} %get-tuple-element.768), channel_id=1, source_target_pairs={{0,8},{8,16},{16,24},{24,0},{1,9},{9,17},{17,25},{25,1},{2,10},{10... | collective-permute-start | bytes 245768 | tf_op jit(solution)/shard_map/while/body/eval_jaxpr/ppermute | solution.py:29
  448.5 5.7 collective-permute-start.1
  449.8 4.5 collective-permute-start.2
  465.1 27.7 %copy-start.6 = (f32[1,1280]{1,0:T(1,128)S(1)}, f32[1,1280]{1,0:T(1,128)}, u32[]{:S(2)}) copy-start(f32[1,1280]{1,0:T(1,128)} %get-tuple-element.859) | copy-start | bytes 15364 | tf_op jit(solution)/shard_map/while
  492.8 56.1 %reduce-scatter.2.cloned.1.call-start = ((), (), s32[]{:S(2)}) async-start(), calls=%async_computation.2 | async-start | bytes 409600 | tf_op jit(solution)/shard_map/while/body/eval_jaxpr/reduce_scatter | solution.py:158
  492.8 14.1 %collective-permute-start = (bf16[1,32,1280]{2,1,0:T(8,128)(2,1)}, bf16[1,32,1280]{2,1,0:T(8,128)(2,1)}, u32[]{:S(2)}, u32[]{:S(2)}) collective-permute-start(bf16[1,32,1280]{2,1,0:T(8,128)(2,1)} %get-tuple-element.768), channel_id=1, source_target_pairs={{0,8},{8,16},{16,24},{24,0},{1,9},{9,17},{17,25},{25,1},{2,10},{10... | collective-permute-start | bytes 245768 | tf_op jit(solution)/shard_map/while/body/eval_jaxpr/ppermute | solution.py:29
  508.0 5.7 collective-permute-start.1
  509.3 4.5 collective-permute-start.2
  552.3 56.1 %reduce-scatter.2.cloned.1.call-start = ((), (), s32[]{:S(2)}) async-start(), calls=%async_computation.2 | async-start | bytes 409600 | tf_op jit(solution)/shard_map/while/body/eval_jaxpr/reduce_scatter | solution.py:158
  552.3 14.2 %collective-permute-start = (bf16[1,32,1280]{2,1,0:T(8,128)(2,1)}, bf16[1,32,1280]{2,1,0:T(8,128)(2,1)}, u32[]{:S(2)}, u32[]{:S(2)}) collective-permute-start(bf16[1,32,1280]{2,1,0:T(8,128)(2,1)} %get-tuple-element.768), channel_id=1, source_target_pairs={{0,8},{8,16},{16,24},{24,0},{1,9},{9,17},{17,25},{25,1},{2,10},{10... | collective-permute-start | bytes 245768 | tf_op jit(solution)/shard_map/while/body/eval_jaxpr/ppermute | solution.py:29
  567.6 5.7 collective-permute-start.1
  568.9 4.5 collective-permute-start.2
  611.8 56.1 %reduce-scatter.2.cloned.1.call-start = ((), (), s32[]{:S(2)}) async-start(), calls=%async_computation.2 | async-start | bytes 409600 | tf_op jit(solution)/shard_map/while/body/eval_jaxpr/reduce_scatter | solution.py:158
  611.8 14.1 %collective-permute-start = (bf16[1,32,1280]{2,1,0:T(8,128)(2,1)}, bf16[1,32,1280]{2,1,0:T(8,128)(2,1)}, u32[]{:S(2)}, u32[]{:S(2)}) collective-permute-start(bf16[1,32,1280]{2,1,0:T(8,128)(2,1)} %get-tuple-element.768), channel_id=1, source_target_pairs={{0,8},{8,16},{16,24},{24,0},{1,9},{9,17},{17,25},{25,1},{2,10},{10... | collective-permute-start | bytes 245768 | tf_op jit(solution)/shard_map/while/body/eval_jaxpr/ppermute | solution.py:29
  627.1 5.7 collective-permute-start.1
  628.4 4.5 collective-permute-start.2
  671.3 39.1 %all-reduce.4.cloned.1.call-start = ((), (), s32[]{:S(2)}) async-start(), calls=%async_computation.1 | async-start | bytes 655360 | tf_op jit(solution)/shard_map/psum | solution.py:34
  (36 other events, 551.4 us)
Sparse Core Ops, SparseCore 0:
  52.4 20.4 reduce-scatter.1
  111.9 20.3 reduce-scatter.1
  171.5 20.2 reduce-scatter.1
  231.0 20.2 reduce-scatter.1
  290.5 20.2 reduce-scatter.1
  350.0 20.2 reduce-scatter.1
  409.6 20.2 reduce-scatter.1
  469.1 20.3 reduce-scatter.1
  528.6 20.2 reduce-scatter.1
  588.1 20.2 reduce-scatter.1
  647.6 20.2 reduce-scatter.1
Sparse Core Ops, SparseCore 1:
  674.1 36.2 all-reduce.3
where the time goes:
time: 725 us; the launch traced here: 719 us
  waiting for transfers between devices  256 us (35%)
  other arithmetic  102 us (14%)
  matrix products  85.6 us (12%)
  blocking collectives  83.5 us (12%)
  local copies, waits for them, and re-layouts  73.6 us (10%)
  starting transfers between devices  65.6 us (9%)
  loops' own time  38.1 us (5%)
  between operations  14.6 us (2%)
    reduce_scatter x11, waiting for transfers between devices, section_heads(): lax.psum_scatter(jnp.dot(attended, out_local, preferred_element_type=jnp....  218 us
    all_gather x11, blocking collectives, section_heads(): normed_all = lax.all_gather(normed, 'tile', axis=0, tiled=True)  83.5 us
    psum x1, waiting for transfers between devices, spread_2(): return lax.psum(jnp.where(mine, shard, jnp.zeros_like(shard)), axis)  38.3 us
    another operation x1, loops' own time, per_device(): final_state = lax.fori_loop(0, tick_total, advance, initial_latent)  38.1 us
    ppermute x11, starting transfers between devices, extended(): lax.ppermute(tail, axis, [(i, (i + 1) % count) for i in range(ends)])  33.4 us
    slice x33, local copies, waits for them, and re-layouts, section_heads(): values_all = jnp.concatenate([projected[:, 2], prompt_pair[:, 1]], axis=0)  31.8 us
    dot_general x11, matrix products, section_heads(): jnp.dot(attended, out_local, preferred_element_type=jnp.float32)  24.9 us
    reduce_sum x22, other arithmetic, pick_integer(): return jnp.sum(jnp.where(hits, int_table, jnp.zeros_like(int_table)))  21.5 us
  transfers between devices with their start and end apart: 45, of which 12 were waited for; matrix products, arithmetic and copies ran while one was open for 17% of the time, Pallas kernels for 0%

commit v1 on v0

--- a/solution.py
+++ b/solution.py
@@ -148,7 +148,14 @@
 
     def section_heads(current, temb_row, prompt_pair):
         mixed, normed = lift_and_mix(current, temb_row)
-        normed_all = lax.all_gather(normed, "tile", axis=0, tiled=True)
+        count_2 = lax.axis_size("tile")
+        forward = [(i_2, (i_2 + 1) % count_2) for i_2 in range(count_2)]
+        shards = [normed]
+        for reach in range(1, count_2):
+            shards = [lax.ppermute(shards[0], "tile", forward), *shards]
+        whole = jnp.concatenate(shards, axis=0)
+        shift = (lax.axis_index("tile") + 1) * shards[-1].shape[0]
+        normed_all = jnp.roll(whole, shift, axis=0)
         projected = jnp.einsum(
             "tc,cjd->tjd", normed_all, qkv_local, preferred_element_type=jnp.float32
         ).astype(jnp.bfloat16)

time: 725 us -> 817 us (1.13)
  blocking collectives: 83.5 us -> 0 us
  waiting for transfers between devices: 256 us -> 322 us
  local copies, waits for them, and re-layouts: 73.6 us -> 132 us
  starting transfers between devices: 65.6 us -> 95 us
  other arithmetic: 102 us -> 122 us
    all_gather x11 -> x0, blocking collectives: 83.5 us -> none  [section_heads(): normed_all = lax.all_gather(normed, 'tile', axis=0, tiled=True)]
    while x66 -> x154, local copies, waits for them, and re-layouts: 0.12 us -> 59.1 us
    ppermute x0 -> x33, waiting for transfers between devices: none -> 48.6 us  [section_heads(): shards = [lax.ppermute(shards[0], 'tile', forward), *shards]]
    ppermute x0 -> x33, starting transfers between devices: none -> 29.4 us  [section_heads(): shards = [lax.ppermute(shards[0], 'tile', forward), *shards]]
    reduce_scatter x11, waiting for transfers between devices: 218 us -> 235 us  [section_heads(): lax.psum_scatter(jnp.dot(attended, out_local, preferred_element_type=jnp....]
  transfers between devices with their start and end apart: 45 -> 78, of which waited for: 12 -> 34; matrix products, arithmetic and copies ran while one was open for 17% -> 16% of each run, Pallas kernels for 0% -> 0%
where the time goes in v1:
time: 817 us; the launch traced here: 808 us
  waiting for transfers between devices  322 us (39%)
  local copies, waits for them, and re-layouts  132 us (16%)
  other arithmetic  122 us (15%)
  starting transfers between devices  95 us (12%)
  matrix products  85.7 us (10%)
  loops' own time  36.2 us (4%)
  between operations  14.6 us (2%)
    reduce_scatter x11, waiting for transfers between devices, section_heads(): lax.psum_scatter(jnp.dot(attended, out_local, preferred_element_type=jnp....  235 us
    while x154, local copies, waits for them, and re-layouts  59.1 us
    ppermute x33, waiting for transfers between devices, section_heads(): shards = [lax.ppermute(shards[0], 'tile', forward), *shards]  48.6 us
    psum x1, waiting for transfers between devices, spread_2(): return lax.psum(jnp.where(mine, shard, jnp.zeros_like(shard)), axis)  38.3 us
    another operation x1, loops' own time, per_device(): final_state = lax.fori_loop(0, tick_total, advance, initial_latent)  36.2 us
    ppermute x11, starting transfers between devices, extended(): lax.ppermute(tail, axis, [(i, (i + 1) % count) for i in range(ends)])  33.4 us
    slice x33, local copies, waits for them, and re-layouts, section_heads(): values_all = jnp.concatenate([projected[:, 2], prompt_pair[:, 1]], axis=0)  31.9 us
    ppermute x33, starting transfers between devices, section_heads(): shards = [lax.ppermute(shards[0], 'tile', forward), *shards]  29.4 us
  transfers between devices with their start and end apart: 78, of which 34 were waited for; matrix products, arithmetic and copies ran while one was open for 16% of the time, Pallas kernels for 0%

profile of v1, /device:TPU:0, one launch (start us, length us, event | category | flops | bytes accessed | tf_op | source)
XLA Modules:
  0.0 808.1 jit_solution(14747870591438969373)
XLA Ops:
  9.0 3.1 copy.18
  14.4 745.9 %while.18 = (s32[]{:T(128)}, bf16[1,32,1280]{2,1,0:T(8,128)(2,1)}, bf16[4,1,32,1280]{3,2,1,0:T(8,128)(2,1)}, s32[]{:T(128)}, pred[]{:T(512)}, /*index=5*/s32[4]{...) while((s32[]{:T(128)}, bf16[1,32,1280]{2,1,0:T(8,128)(2,1)}, ...), condition=%wide.region_10.11_spmd.clone, body=%wide.region_2.10_spmd.clone.sunk | while | flops 659035008 | bytes 29193816 | solution.py:213
  14.4 3.1 collective-permute-start
  27.8 3.0 collective-permute-start.2
  34.2 2.7 collective-permute-done.3
  56.6 2.3 convolution_convert_fusion.11
  59.5 21.5 %reduce-scatter.2.cloned.1.call-done = bf16[32,1280]{1,0:T(8,128)(2,1)} async-done(((bf16[128,1280]{1,0:T(8,128)(2,1)}), bf16[32,1280]{1,0:T(8,128)(2,1)}) %reduce-scatter.2.cloned.1.call-update) | async-done | bytes 81936 | tf_op jit(solution)/shard_map/while/body/eval_jaxpr/reduce_scatter | solution.py:165
  96.1 3.0 collective-permute-start.2
  101.9 3.2 collective-permute-done.3
  124.4 2.3 convolution_convert_fusion.11
  127.2 21.3 %reduce-scatter.2.cloned.1.call-done = bf16[32,1280]{1,0:T(8,128)(2,1)} async-done(((bf16[128,1280]{1,0:T(8,128)(2,1)}), bf16[32,1280]{1,0:T(8,128)(2,1)}) %reduce-scatter.2.cloned.1.call-update) | async-done | bytes 81936 | tf_op jit(solution)/shard_map/while/body/eval_jaxpr/reduce_scatter | solution.py:165
  163.7 3.0 collective-permute-start.2
  169.5 3.2 collective-permute-done.3
  192.0 2.3 convolution_convert_fusion.11
  194.8 21.3 %reduce-scatter.2.cloned.1.call-done = bf16[32,1280]{1,0:T(8,128)(2,1)} async-done(((bf16[128,1280]{1,0:T(8,128)(2,1)}), bf16[32,1280]{1,0:T(8,128)(2,1)}) %reduce-scatter.2.cloned.1.call-update) | async-done | bytes 81936 | tf_op jit(solution)/shard_map/while/body/eval_jaxpr/reduce_scatter | solution.py:165
  231.3 3.0 collective-permute-start.2
  237.1 3.2 collective-permute-done.3
  259.5 2.3 convolution_convert_fusion.11
  262.4 21.3 %reduce-scatter.2.cloned.1.call-done = bf16[32,1280]{1,0:T(8,128)(2,1)} async-done(((bf16[128,1280]{1,0:T(8,128)(2,1)}), bf16[32,1280]{1,0:T(8,128)(2,1)}) %reduce-scatter.2.cloned.1.call-update) | async-done | bytes 81936 | tf_op jit(solution)/shard_map/while/body/eval_jaxpr/reduce_scatter | solution.py:165
  298.9 3.0 collective-permute-start.2
  304.7 3.2 collective-permute-done.3
  327.1 2.3 convolution_convert_fusion.11
  330.0 21.3 %reduce-scatter.2.cloned.1.call-done = bf16[32,1280]{1,0:T(8,128)(2,1)} async-done(((bf16[128,1280]{1,0:T(8,128)(2,1)}), bf16[32,1280]{1,0:T(8,128)(2,1)}) %reduce-scatter.2.cloned.1.call-update) | async-done | bytes 81936 | tf_op jit(solution)/shard_map/while/body/eval_jaxpr/reduce_scatter | solution.py:165
  366.5 3.0 collective-permute-start.2
  372.3 3.2 collective-permute-done.3
  394.7 2.3 convolution_convert_fusion.11
  397.6 21.3 %reduce-scatter.2.cloned.1.call-done = bf16[32,1280]{1,0:T(8,128)(2,1)} async-done(((bf16[128,1280]{1,0:T(8,128)(2,1)}), bf16[32,1280]{1,0:T(8,128)(2,1)}) %reduce-scatter.2.cloned.1.call-update) | async-done | bytes 81936 | tf_op jit(solution)/shard_map/while/body/eval_jaxpr/reduce_scatter | solution.py:165
  434.1 3.0 collective-permute-start.2
  439.9 3.2 collective-permute-done.3
  462.3 2.3 convolution_convert_fusion.11
  465.2 21.3 %reduce-scatter.2.cloned.1.call-done = bf16[32,1280]{1,0:T(8,128)(2,1)} async-done(((bf16[128,1280]{1,0:T(8,128)(2,1)}), bf16[32,1280]{1,0:T(8,128)(2,1)}) %reduce-scatter.2.cloned.1.call-update) | async-done | bytes 81936 | tf_op jit(solution)/shard_map/while/body/eval_jaxpr/reduce_scatter | solution.py:165
  501.7 3.0 collective-permute-start.2
  507.5 3.2 collective-permute-done.3
  530.0 2.3 convolution_convert_fusion.11
  532.8 21.3 %reduce-scatter.2.cloned.1.call-done = bf16[32,1280]{1,0:T(8,128)(2,1)} async-done(((bf16[128,1280]{1,0:T(8,128)(2,1)}), bf16[32,1280]{1,0:T(8,128)(2,1)}) %reduce-scatter.2.cloned.1.call-update) | async-done | bytes 81936 | tf_op jit(solution)/shard_map/while/body/eval_jaxpr/reduce_scatter | solution.py:165
  569.3 3.0 collective-permute-start.2
  575.1 3.2 collective-permute-done.3
  597.5 2.3 convolution_convert_fusion.11
  600.4 21.3 %reduce-scatter.2.cloned.1.call-done = bf16[32,1280]{1,0:T(8,128)(2,1)} async-done(((bf16[128,1280]{1,0:T(8,128)(2,1)}), bf16[32,1280]{1,0:T(8,128)(2,1)}) %reduce-scatter.2.cloned.1.call-update) | async-done | bytes 81936 | tf_op jit(solution)/shard_map/while/body/eval_jaxpr/reduce_scatter | solution.py:165
  636.9 3.0 collective-permute-start.2
  642.7 3.2 collective-permute-done.3
  665.1 2.3 convolution_convert_fusion.11
  668.0 21.3 %reduce-scatter.2.cloned.1.call-done = bf16[32,1280]{1,0:T(8,128)(2,1)} async-done(((bf16[128,1280]{1,0:T(8,128)(2,1)}), bf16[32,1280]{1,0:T(8,128)(2,1)}) %reduce-scatter.2.cloned.1.call-update) | async-done | bytes 81936 | tf_op jit(solution)/shard_map/while/body/eval_jaxpr/reduce_scatter | solution.py:165
  704.5 3.0 collective-permute-start.2
  710.3 3.2 collective-permute-done.3
  732.7 2.3 convolution_convert_fusion.11
  735.6 21.3 %reduce-scatter.2.cloned.1.call-done = bf16[32,1280]{1,0:T(8,128)(2,1)} async-done(((bf16[128,1280]{1,0:T(8,128)(2,1)}), bf16[32,1280]{1,0:T(8,128)(2,1)}) %reduce-scatter.2.cloned.1.call-update) | async-done | bytes 81936 | tf_op jit(solution)/shard_map/while/body/eval_jaxpr/reduce_scatter | solution.py:165
  761.0 38.3 %all-reduce.4.cloned.1.call-done = bf16[4,1,32,1280]{3,2,1,0:T(8,128)(2,1)} async-done(((bf16[4,1,32,1280]{3,2,1,0:T(8,128)(2,1)}), bf16[4,1,32,1280]{3,2,1,0:T(8,128)(2,1)}) %all-reduce.4.cloned.1.call-update) | async-done | bytes 327696 | tf_op jit(solution)/shard_map/psum | solution.py:34
  (611 shorter events, 385.6 us)
Async XLA Ops:
  14.4 66.7 %reduce-scatter.2.cloned.1.call-start = ((), (), s32[]{:S(2)}) async-start(), calls=%async_computation.2 | async-start | bytes 409600 | tf_op jit(solution)/shard_map/while/body/eval_jaxpr/reduce_scatter | solution.py:165
  14.4 11.1 %collective-permute-start = (bf16[1,32,1280]{2,1,0:T(8,128)(2,1)}, bf16[1,32,1280]{2,1,0:T(8,128)(2,1)S(1)}, u32[]{:S(2)}, u32[]{:S(2)}) collective-permute-start(bf16[1,32,1280]{2,1,0:T(8,128)(2,1)} %get-tuple-element.776), channel_id=1, source_target_pairs={{0,8},{8,16},{16,24},{24,0},{1,9},{9,17},{17,25},{25,1},{2,10},{10... | collective-permute-start | bytes 245768 | tf_op jit(solution)/shard_map/while/body/eval_jaxpr/ppermute | solution.py:29
  26.5 5.7 collective-permute-start.1
  27.8 4.4 collective-permute-start.2
  40.8 4.8 collective-permute-start.5
  84.3 64.2 %reduce-scatter.2.cloned.1.call-start = ((), (), s32[]{:S(2)}) async-start(), calls=%async_computation.2 | async-start | bytes 409600 | tf_op jit(solution)/shard_map/while/body/eval_jaxpr/reduce_scatter | solution.py:165
  84.3 9.5 %collective-permute-start = (bf16[1,32,1280]{2,1,0:T(8,128)(2,1)}, bf16[1,32,1280]{2,1,0:T(8,128)(2,1)S(1)}, u32[]{:S(2)}, u32[]{:S(2)}) collective-permute-start(bf16[1,32,1280]{2,1,0:T(8,128)(2,1)} %get-tuple-element.776), channel_id=1, source_target_pairs={{0,8},{8,16},{16,24},{24,0},{1,9},{9,17},{17,25},{25,1},{2,10},{10... | collective-permute-start | bytes 245768 | tf_op jit(solution)/shard_map/while/body/eval_jaxpr/ppermute | solution.py:29
  94.8 5.7 collective-permute-start.1
  96.1 4.4 collective-permute-start.2
  109.1 4.3 collective-permute-start.5
  151.9 64.2 %reduce-scatter.2.cloned.1.call-start = ((), (), s32[]{:S(2)}) async-start(), calls=%async_computation.2 | async-start | bytes 409600 | tf_op jit(solution)/shard_map/while/body/eval_jaxpr/reduce_scatter | solution.py:165
  151.9 9.5 %collective-permute-start = (bf16[1,32,1280]{2,1,0:T(8,128)(2,1)}, bf16[1,32,1280]{2,1,0:T(8,128)(2,1)S(1)}, u32[]{:S(2)}, u32[]{:S(2)}) collective-permute-start(bf16[1,32,1280]{2,1,0:T(8,128)(2,1)} %get-tuple-element.776), channel_id=1, source_target_pairs={{0,8},{8,16},{16,24},{24,0},{1,9},{9,17},{17,25},{25,1},{2,10},{10... | collective-permute-start | bytes 245768 | tf_op jit(solution)/shard_map/while/body/eval_jaxpr/ppermute | solution.py:29
  162.4 5.7 collective-permute-start.1
  163.7 4.4 collective-permute-start.2
  219.5 64.2 %reduce-scatter.2.cloned.1.call-start = ((), (), s32[]{:S(2)}) async-start(), calls=%async_computation.2 | async-start | bytes 409600 | tf_op jit(solution)/shard_map/while/body/eval_jaxpr/reduce_scatter | solution.py:165
  219.5 9.5 %collective-permute-start = (bf16[1,32,1280]{2,1,0:T(8,128)(2,1)}, bf16[1,32,1280]{2,1,0:T(8,128)(2,1)S(1)}, u32[]{:S(2)}, u32[]{:S(2)}) collective-permute-start(bf16[1,32,1280]{2,1,0:T(8,128)(2,1)} %get-tuple-element.776), channel_id=1, source_target_pairs={{0,8},{8,16},{16,24},{24,0},{1,9},{9,17},{17,25},{25,1},{2,10},{10... | collective-permute-start | bytes 245768 | tf_op jit(solution)/shard_map/while/body/eval_jaxpr/ppermute | solution.py:29
  230.0 5.7 collective-permute-start.1
  231.3 4.4 collective-permute-start.2
  287.1 64.3 %reduce-scatter.2.cloned.1.call-start = ((), (), s32[]{:S(2)}) async-start(), calls=%async_computation.2 | async-start | bytes 409600 | tf_op jit(solution)/shard_map/while/body/eval_jaxpr/reduce_scatter | solution.py:165
  287.1 9.5 %collective-permute-start = (bf16[1,32,1280]{2,1,0:T(8,128)(2,1)}, bf16[1,32,1280]{2,1,0:T(8,128)(2,1)S(1)}, u32[]{:S(2)}, u32[]{:S(2)}) collective-permute-start(bf16[1,32,1280]{2,1,0:T(8,128)(2,1)} %get-tuple-element.776), channel_id=1, source_target_pairs={{0,8},{8,16},{16,24},{24,0},{1,9},{9,17},{17,25},{25,1},{2,10},{10... | collective-permute-start | bytes 245768 | tf_op jit(solution)/shard_map/while/body/eval_jaxpr/ppermute | solution.py:29
  297.6 5.7 collective-permute-start.1
  298.9 4.4 collective-permute-start.2
  354.7 64.2 %reduce-scatter.2.cloned.1.call-start = ((), (), s32[]{:S(2)}) async-start(), calls=%async_computation.2 | async-start | bytes 409600 | tf_op jit(solution)/shard_map/while/body/eval_jaxpr/reduce_scatter | solution.py:165
  354.7 9.5 %collective-permute-start = (bf16[1,32,1280]{2,1,0:T(8,128)(2,1)}, bf16[1,32,1280]{2,1,0:T(8,128)(2,1)S(1)}, u32[]{:S(2)}, u32[]{:S(2)}) collective-permute-start(bf16[1,32,1280]{2,1,0:T(8,128)(2,1)} %get-tuple-element.776), channel_id=1, source_target_pairs={{0,8},{8,16},{16,24},{24,0},{1,9},{9,17},{17,25},{25,1},{2,10},{10... | collective-permute-start | bytes 245768 | tf_op jit(solution)/shard_map/while/body/eval_jaxpr/ppermute | solution.py:29
  365.2 5.7 collective-permute-start.1
  366.5 4.4 collective-permute-start.2
  422.3 64.2 %reduce-scatter.2.cloned.1.call-start = ((), (), s32[]{:S(2)}) async-start(), calls=%async_computation.2 | async-start | bytes 409600 | tf_op jit(solution)/shard_map/while/body/eval_jaxpr/reduce_scatter | solution.py:165
  422.3 9.5 %collective-permute-start = (bf16[1,32,1280]{2,1,0:T(8,128)(2,1)}, bf16[1,32,1280]{2,1,0:T(8,128)(2,1)S(1)}, u32[]{:S(2)}, u32[]{:S(2)}) collective-permute-start(bf16[1,32,1280]{2,1,0:T(8,128)(2,1)} %get-tuple-element.776), channel_id=1, source_target_pairs={{0,8},{8,16},{16,24},{24,0},{1,9},{9,17},{17,25},{25,1},{2,10},{10... | collective-permute-start | bytes 245768 | tf_op jit(solution)/shard_map/while/body/eval_jaxpr/ppermute | solution.py:29
  432.8 5.7 collective-permute-start.1
  434.1 4.4 collective-permute-start.2
  489.9 64.2 %reduce-scatter.2.cloned.1.call-start = ((), (), s32[]{:S(2)}) async-start(), calls=%async_computation.2 | async-start | bytes 409600 | tf_op jit(solution)/shard_map/while/body/eval_jaxpr/reduce_scatter | solution.py:165
  489.9 9.5 %collective-permute-start = (bf16[1,32,1280]{2,1,0:T(8,128)(2,1)}, bf16[1,32,1280]{2,1,0:T(8,128)(2,1)S(1)}, u32[]{:S(2)}, u32[]{:S(2)}) collective-permute-start(bf16[1,32,1280]{2,1,0:T(8,128)(2,1)} %get-tuple-element.776), channel_id=1, source_target_pairs={{0,8},{8,16},{16,24},{24,0},{1,9},{9,17},{17,25},{25,1},{2,10},{10... | collective-permute-start | bytes 245768 | tf_op jit(solution)/shard_map/while/body/eval_jaxpr/ppermute | solution.py:29
  500.4 5.7 collective-permute-start.1
  501.7 4.4 collective-permute-start.2
  557.5 64.3 %reduce-scatter.2.cloned.1.call-start = ((), (), s32[]{:S(2)}) async-start(), calls=%async_computation.2 | async-start | bytes 409600 | tf_op jit(solution)/shard_map/while/body/eval_jaxpr/reduce_scatter | solution.py:165
  557.5 9.5 %collective-permute-start = (bf16[1,32,1280]{2,1,0:T(8,128)(2,1)}, bf16[1,32,1280]{2,1,0:T(8,128)(2,1)S(1)}, u32[]{:S(2)}, u32[]{:S(2)}) collective-permute-start(bf16[1,32,1280]{2,1,0:T(8,128)(2,1)} %get-tuple-element.776), channel_id=1, source_target_pairs={{0,8},{8,16},{16,24},{24,0},{1,9},{9,17},{17,25},{25,1},{2,10},{10... | collective-permute-start | bytes 245768 | tf_op jit(solution)/shard_map/while/body/eval_jaxpr/ppermute | solution.py:29
  568.0 5.7 collective-permute-start.1
  569.3 4.4 collective-permute-start.2
  625.1 64.2 %reduce-scatter.2.cloned.1.call-start = ((), (), s32[]{:S(2)}) async-start(), calls=%async_computation.2 | async-start | bytes 409600 | tf_op jit(solution)/shard_map/while/body/eval_jaxpr/reduce_scatter | solution.py:165
  625.1 9.5 %collective-permute-start = (bf16[1,32,1280]{2,1,0:T(8,128)(2,1)}, bf16[1,32,1280]{2,1,0:T(8,128)(2,1)S(1)}, u32[]{:S(2)}, u32[]{:S(2)}) collective-permute-start(bf16[1,32,1280]{2,1,0:T(8,128)(2,1)} %get-tuple-element.776), channel_id=1, source_target_pairs={{0,8},{8,16},{16,24},{24,0},{1,9},{9,17},{17,25},{25,1},{2,10},{10... | collective-permute-start | bytes 245768 | tf_op jit(solution)/shard_map/while/body/eval_jaxpr/ppermute | solution.py:29
  635.6 5.7 collective-permute-start.1
  636.9 4.4 collective-permute-start.2
  692.7 64.3 %reduce-scatter.2.cloned.1.call-start = ((), (), s32[]{:S(2)}) async-start(), calls=%async_computation.2 | async-start | bytes 409600 | tf_op jit(solution)/shard_map/while/body/eval_jaxpr/reduce_scatter | solution.py:165
  692.7 9.5 %collective-permute-start = (bf16[1,32,1280]{2,1,0:T(8,128)(2,1)}, bf16[1,32,1280]{2,1,0:T(8,128)(2,1)S(1)}, u32[]{:S(2)}, u32[]{:S(2)}) collective-permute-start(bf16[1,32,1280]{2,1,0:T(8,128)(2,1)} %get-tuple-element.776), channel_id=1, source_target_pairs={{0,8},{8,16},{16,24},{24,0},{1,9},{9,17},{17,25},{25,1},{2,10},{10... | collective-permute-start | bytes 245768 | tf_op jit(solution)/shard_map/while/body/eval_jaxpr/ppermute | solution.py:29
  703.2 5.7 collective-permute-start.1
  704.5 4.4 collective-permute-start.2
  717.4 4.3 collective-permute-start.5
  760.3 39.1 %all-reduce.4.cloned.1.call-start = ((), (), s32[]{:S(2)}) async-start(), calls=%async_computation.1 | async-start | bytes 655360 | tf_op jit(solution)/shard_map/psum | solution.py:34
  (79 other events, 731.5 us)
Sparse Core Ops, SparseCore 0:
  59.0 21.9 reduce-scatter.1
  126.8 21.7 reduce-scatter.1
  194.4 21.7 reduce-scatter.1
  261.9 21.7 reduce-scatter.1
  329.5 21.7 reduce-scatter.1
  397.2 21.7 reduce-scatter.1
  464.7 21.7 reduce-scatter.1
  532.4 21.7 reduce-scatter.1
  599.9 21.7 reduce-scatter.1
  667.5 21.7 reduce-scatter.1
  735.1 21.7 reduce-scatter.1
Sparse Core Ops, SparseCore 1:
  763.1 36.2 all-reduce.3
